TPU v7x, 128 devices: a whole 4x4x4 slice. The times are simulated.
128 devices in a mesh: grp: 4 (over y_hi, core), row: 32 (over y_lo, z, x).
Axes of the slice: x: 4, y: 4 (y_hi: 2, y_lo: 2; y = y_hi * 2 + y_lo), z: 4, core: 2. Of those that a mesh axis runs over, the one named last changes fastest.
Arguments:
- landmarks: bfloat16 [4096, 1024], P(('grp', 'row')), may hold values from -6.5 to 6.5
- initial_basis: bfloat16 [4096, 256], P(('grp', 'row')), may hold values from -0.09375 to 0.09375
- points: bfloat16 [131072, 1024], P(('grp', 'row')), may hold values from -6.5 to 6.5
Outputs:
- basis: float32 [4096, 256], P(('grp', 'row'))
- coords: float32 [131072, 256], P(('grp', 'row'))
All inputs are finite; a program needn't handle non-finite values.
Results may differ from a plain program's by a relative error of at most 0.0057.
Values may be sent and summed in bfloat16 or wider, within the bound.
A program may use at most 128 MiB of HBM per device.

v0:
```python
import math
import jax
import jax.numpy as jnp
from jax import lax
from jax.sharding import PartitionSpec as P

ITERS = 2
spread = 0.25


def laid_out(blocks, dim):
    blocks = jnp.moveaxis(blocks, 0, dim)
    shape = blocks.shape
    return blocks.reshape(*shape[:dim], shape[dim] * shape[dim + 1], *shape[dim + 2 :])


def copy_for_each(x, axis):
    devices = lax.axis_size(axis)
    return lax.all_to_all(jnp.broadcast_to(x[None], (devices, *x.shape)), axis, 0, 0, tiled=True)


def collect(x, axis, dim):
    return laid_out(copy_for_each(x, axis), dim)


def of_everyone(x, axis):
    return copy_for_each(x, axis).sum(axis=0)


def in_blocks(x, dim, devices):
    shape = x.shape
    blocks = x.reshape(*shape[:dim], devices, shape[dim] // devices, *shape[dim + 1 :])
    return jnp.moveaxis(blocks, dim, 0)


def sum_at_owner(x, axis, dim):
    devices = lax.axis_size(axis)
    blocks = lax.all_to_all(in_blocks(x, dim, devices), axis, 0, 0, tiled=True)
    return jnp.sum(blocks, axis=0)


def side_by_side(arrays, axis, dim, along):
    columns = [a.reshape(*a.shape[:along], -1) for a in arrays]
    both = jnp.concatenate(columns, axis=along)
    out, at, gathered = (lax.psum_scatter(both, axis, scatter_dimension=dim, tiled=True), 0, [])
    for a, column in zip(arrays, columns):
        share = out[..., at : at + column.shape[along]]
        gathered.append(share.reshape(*share.shape[:along], *a.shape[along:]))
        at += column.shape[along]
    return tuple(gathered)


def squared_rows(rows):
    return jnp.sum(jnp.square(rows.astype(jnp.float32)), axis=1)


def pair_kernel(left, right):
    inner = lax.dot_general(
        left, right, (((1,), (1,)), ((), ())), preferred_element_type=jnp.float32
    )
    dist = squared_rows(left)[:, None] + squared_rows(right)[None, :] - 2.0 * inner
    return jnp.exp(-dist / (spread * left.shape[1]))


def point_terms(anchors, spectral_rows, members, member_sq):
    inner = lax.dot_general(
        anchors, members, (((1,), (1,)), ((), ())), preferred_element_type=jnp.float32
    )
    dist = squared_rows(anchors)[:, None] + member_sq[None, :] - 2.0 * inner
    kernel_part = jnp.exp(-dist / (spread * anchors.shape[1]))
    degree_part = jnp.sum(kernel_part, axis=0)
    numer_part = lax.dot_general(
        kernel_part.astype(jnp.bfloat16),
        spectral_rows,
        (((0,), (0,)), ((), ())),
        preferred_element_type=jnp.float32,
    )
    return (numer_part, degree_part)


def body(landmarks, initial_basis, points):
    local_rows = landmarks.shape[0]
    total = local_rows * lax.axis_size("grp") * lax.axis_size("row")
    row_index = lax.axis_index("row")
    group_rows = lax.all_gather(landmarks, "row", axis=0, tiled=True)
    cross_rows = collect(landmarks, "grp", 0)
    land_kernel = pair_kernel(group_rows, cross_rows)
    group_degree = of_everyone(jnp.sum(land_kernel, axis=1), "row")
    own_degree = lax.dynamic_slice_in_dim(group_degree, row_index * local_rows, local_rows, 0)
    cross_degree = collect(own_degree, "grp", 0)
    row_scale = 1.0 / jnp.sqrt(group_degree)
    column_scale = 1.0 / jnp.sqrt(cross_degree)
    affinity = (land_kernel * row_scale[:, None] * column_scale[None, :]).astype(jnp.bfloat16)
    current = initial_basis
    for step in range(ITERS):
        cross_basis = collect(current, "grp", 0)
        image = sum_at_owner(
            jnp.dot(affinity, cross_basis, preferred_element_type=jnp.float32), "row", 0
        )
        gram = lax.psum(jnp.dot(image.T, image, precision=lax.Precision.HIGHEST), ("grp", "row"))
        lower = jnp.linalg.cholesky(gram)
        ortho = jax.scipy.linalg.solve_triangular(lower, image.T, lower=True).T
        current = ortho.astype(jnp.bfloat16)
    lam = jnp.diagonal(lower)
    own_scale = 1.0 / jnp.sqrt(own_degree)
    spectral = (ortho * own_scale[:, None] / lam[None, :]).astype(jnp.bfloat16)
    group_spectral = collect(spectral, "row", 0)
    cross_points = lax.all_gather(points, "grp", axis=0, tiled=True)
    numer_part, degree_part = point_terms(
        group_rows, group_spectral, cross_points, squared_rows(cross_points)
    )
    numer, degree = side_by_side((numer_part, degree_part), "grp", 0, 1)
    coords = numer / jnp.sqrt(degree)[:, None] * math.sqrt(total)
    return (ortho, coords)


def solution(mesh):
    in_specs = (P(("grp", "row"), None), P(("grp", "row"), None), P(("grp", "row"), None))
    out_specs = (P(("grp", "row"), None), P(("grp", "row"), None))
    return jax.shard_map(body, mesh=mesh, in_specs=in_specs, out_specs=out_specs, check_vma=False)
```

profile of v0, /device:TPU:1, one launch (start us, length us, event | category | flops | bytes accessed | tf_op | source)
XLA Modules:
  0.0 810.1 jit_solution(4297087186044760652)
XLA Ops:
  8.0 0.7 all-gather.3.cloned.1.call-update
  8.7 0.9 broadcast_in_dim.14
  9.6 12.2 %all_to_all.42 = bf16[4,32,1024]{2,1,0:T(8,128)(2,1)S(1)} all-to-all(bf16[4,32,1024]{2,1,0:T(8,128)(2,1)S(1)} %broadcast_in_dim.14), channel_id=1, replica_groups=mesh['grp'=4,'row'=32] {'grp'}, dimensions={0} | all-to-all | bytes 524288 | tf_op jit(solution)/shard_map/all_to_all | solution.py:19
  22.0 122.9 %all-gather.3.cloned.1.call-done = bf16[1024,1024]{1,0:T(8,128)(2,1)} async-done(((bf16[32,1024]{1,0:T(8,128)(2,1)}), bf16[1024,1024]{1,0:T(8,128)(2,1)}) %all-gather.3.cloned.1.call-update) | async-done | bytes 2097168 | tf_op jit(solution)/shard_map/all_gather | solution.py:85
  145.0 2.1 multiply_reduce_fusion.1
  147.0 2.4 fusion.38
  149.4 0.7 broadcast_in_dim.15
  150.1 6.2 all-to-all-start.1
  156.4 7.3 all-to-all-done.1
  163.9 0.6 broadcast_in_dim.16
  164.4 28.1 %all-to-all-start.2 = ((f32[4,1,32]{2,1,0:T(1,128)}), f32[4,1,32]{2,1,0:T(1,128)S(1)}, u32[]{:S(2)}, u32[]{:S(2)}) async-start(f32[4,1,32]{2,1,0:T(1,128)} %broadcast_in_dim.16), calls=%async_computation.2 | async-start | bytes 4096 | tf_op jit(solution)/shard_map/all_to_all | solution.py:19
  192.6 4.5 all-to-all-done.2
  197.1 1.4 broadcast_in_dim.17
  198.4 3.9 all-to-all-start.3
  202.7 4.4 all-to-all-done.3
  207.1 0.3 fusion.39
  207.4 19.0 %all_to_all.44 = f32[32,32,256]{2,1,0:T(8,128)S(1)} all-to-all(f32[32,32,256]{2,1,0:T(8,128)S(1)} %fusion.39), channel_id=1, replica_groups=mesh['grp'=4,'row'=32] {'row'}, dimensions={0} | all-to-all | bytes 2097152 | tf_op jit(solution)/shard_map/all_to_all | solution.py:38
  226.5 1.1 fusion.40
  227.7 0.5 all-reduce.6.cloned.1.call-start
  228.2 140.3 %all-reduce.4.cloned.1.call-done = f32[256,256]{0,1:T(8,128)} async-done(((f32[256,256]{0,1:T(8,128)}), f32[256,256]{0,1:T(8,128)}) %all-reduce.4.cloned.1.call-update) | async-done | bytes 262160 | tf_op jit(solution)/shard_map/psum | solution.py:100
  368.5 1.1 copy.27
  369.6 1.0 fusion.10
  370.6 11.7 %cholesky.130 = f32[128,128]{1,0:T(8,128)S(1)} custom-call(f32[128,128]{1,0:T(8,128)S(1)} %cholesky.194), custom_call_target="Cholesky" | custom-call | tf_op jit(solution)/shard_map/jit(cholesky)/cholesky | solution.py:101
  382.4 9.8 %custom-call.15 = f32[1,128,128]{1,2,0:T(8,128)S(1)} custom-call(f32[1,128,128]{2,1,0:T(8,128)S(1)} %get-tuple-element.63), custom_call_target="InvertDiagBlocksLowerTriangular" | custom-call | tf_op jit(solution)/shard_map/jit(cholesky)/cholesky | solution.py:101
  392.7 11.7 %cholesky.147 = f32[128,128]{1,0:T(8,128)S(1)} custom-call(f32[128,128]{1,0:T(8,128)S(1)} %convolution_subtract_fusion.1), custom_call_target="Cholesky" | custom-call | tf_op jit(solution)/shard_map/jit(cholesky)/cholesky | solution.py:101
  404.4 0.7 compare_reduce_fusion.2
  406.6 4.2 while.4
  406.8 0.6 fusion.66
  407.3 1.4 bitcast_dynamic-update-slice_fusion.4
  408.8 0.6 fusion.66
  409.4 1.4 bitcast_dynamic-update-slice_fusion.4
  410.8 19.7 %custom-call.16 = f32[2,128,128]{1,2,0:T(8,128)S(1)} custom-call(f32[2,128,128]{2,1,0:T(8,128)S(1)} %get-tuple-element.18), custom_call_target="InvertDiagBlocksLowerTriangular" | custom-call | tf_op jit(solution)/shard_map/jit(_solve_triangular)/triangular_solve | solution.py:102
  431.1 8.7 %all_to_all.43 = bf16[4,32,256]{2,1,0:T(8,128)(2,1)S(1)} all-to-all(bf16[4,32,256]{2,1,0:T(8,128)(2,1)S(1)} %broadcast_in_dim.18), channel_id=1, replica_groups=mesh['grp'=4,'row'=32] {'grp'}, dimensions={0} | all-to-all | bytes 131072 | tf_op jit(solution)/shard_map/all_to_all | solution.py:19
  439.8 0.3 fusion.41
  440.1 19.6 %all_to_all.45 = f32[32,32,256]{2,1,0:T(8,128)S(1)} all-to-all(f32[32,32,256]{2,1,0:T(8,128)S(1)} %fusion.41), channel_id=1, replica_groups=mesh['grp'=4,'row'=32] {'row'}, dimensions={0} | all-to-all | bytes 2097152 | tf_op jit(solution)/shard_map/all_to_all | solution.py:38
  459.7 1.1 fusion.42
  460.9 0.5 all-gather.5.cloned.1.call-update
  461.5 183.1 %all-reduce.6.cloned.1.call-done = f32[256,256]{0,1:T(8,128)} async-done(((f32[256,256]{0,1:T(8,128)}), f32[256,256]{0,1:T(8,128)}) %all-reduce.6.cloned.1.call-update) | async-done | bytes 262160 | tf_op jit(solution)/shard_map/psum | solution.py:100
  644.5 1.1 copy.29
  645.6 1.0 fusion.9
  646.6 11.7 %cholesky.164 = f32[128,128]{1,0:T(8,128)S(1)} custom-call(f32[128,128]{1,0:T(8,128)S(1)} %cholesky.197), custom_call_target="Cholesky" | custom-call | tf_op jit(solution)/shard_map/jit(cholesky)/cholesky | solution.py:101
  658.4 9.8 %custom-call.17 = f32[1,128,128]{1,2,0:T(8,128)S(1)} custom-call(f32[1,128,128]{2,1,0:T(8,128)S(1)} %get-tuple-element.59), custom_call_target="InvertDiagBlocksLowerTriangular" | custom-call | tf_op jit(solution)/shard_map/jit(cholesky)/cholesky | solution.py:101
  668.7 11.7 %cholesky.181 = f32[128,128]{1,0:T(8,128)S(1)} custom-call(f32[128,128]{1,0:T(8,128)S(1)} %convolution_subtract_fusion), custom_call_target="Cholesky" | custom-call | tf_op jit(solution)/shard_map/jit(cholesky)/cholesky | solution.py:101
  680.4 0.6 compare_reduce_fusion.1
  681.1 0.6 compare_reduce_fusion
  683.1 4.2 while.5
  683.3 0.6 fusion.67
  683.9 1.4 bitcast_dynamic-update-slice_fusion.5
  685.3 0.6 fusion.67
  685.9 1.4 bitcast_dynamic-update-slice_fusion.5
  687.3 19.7 %custom-call.18 = f32[2,128,128]{1,2,0:T(8,128)S(1)} custom-call(f32[2,128,128]{2,1,0:T(8,128)S(1)} %get-tuple-element.19), custom_call_target="InvertDiagBlocksLowerTriangular" | custom-call | tf_op jit(solution)/shard_map/jit(_solve_triangular)/triangular_solve | solution.py:102
  707.0 2.3 gather_fusion
  709.9 0.6 divide_convert_fusion
  710.5 0.9 broadcast_in_dim.19
  711.4 5.0 all-to-all-start.7
  716.5 5.2 multiply_reduce_fusion
  721.7 0.5 copy-done
  722.2 13.9 %fusion = (f32[4096]{0:T(1024)S(1)}, f32[1024,4096]{1,0:T(8,128)}) fusion(f32[4096]{0:T(1024)S(1)} %multiply_reduce_fusion, f32[1024]{0:T(1024)S(1)} %multiply_reduce_fusion.1, bf16[1024,1024]{1,0:T(8,128)(2,1)S(1)} %copy-done.1, bf16[4096,1024]{1,0:T(8,128)(2,1)S(1)} %copy-done), kind=kOutput, calls=%fused_computation.7 | convolution fusion | flops 8615096320 | bytes 27299840 | tf_op jit(solution)/shard_map/dot_general | solution.py:66
  736.1 8.2 %fusion.2 = f32[4096,256]{0,1:T(8,128)S(1)} fusion(bf16[1024,256]{1,0:T(8,128)(2,1)S(1)} %bitcast.102, f32[1024,4096]{1,0:T(8,128)} %get-tuple-element.71, f32[4096]{0:T(1024)S(1)} %multiply_reduce_fusion, f32[1024]{0:T(1024)S(1)} %multiply_reduce_fusion.1), kind=kOutput, calls=%fused_computation.9 | convolution fusion | flops 2172649472 | bytes 21516288 | tf_op jit(solution)/shard_map/dot_general | solution.py:72
  744.3 2.3 pad_maximum_fusion
  746.6 52.7 %reduce-scatter.2.cloned.1.call-done = f32[1024,257]{0,1:T(8,128)} async-done(((f32[4096,257]{0,1:T(8,128)}), f32[1024,257]{0,1:T(8,128)}) %reduce-scatter.2.cloned.1.call-update) | async-done | bytes 1052688 | tf_op jit(solution)/shard_map/reduce_scatter | solution.py:45
  799.3 0.8 slice_sqrt_fusion
  800.1 1.4 fusion.8
  801.5 1.3 copy.30
  (53 shorter events, 3.5 us)
Async XLA Ops:
  8.0 137.0 %all-gather.3.cloned.1.call-start = ((), (), s32[]{:S(2)}) async-start(), calls=%async_computation.9 | async-start | bytes 2162688 | tf_op jit(solution)/shard_map/all_gather | solution.py:85
  150.1 13.5 %all-to-all-start.1 = ((f32[32,1,1024]{2,1,0:T(1,128)}), f32[32,1,1024]{2,1,0:T(1,128)S(1)}, u32[]{:S(2)}, u32[]{:S(2)}) async-start(f32[32,1,1024]{2,1,0:T(1,128)} %broadcast_in_dim.15), calls=%async_computation.1 | async-start | bytes 262144 | tf_op jit(solution)/shard_map/all_to_all | solution.py:19
  164.4 32.6 %all-to-all-start.2 = ((f32[4,1,32]{2,1,0:T(1,128)}), f32[4,1,32]{2,1,0:T(1,128)S(1)}, u32[]{:S(2)}, u32[]{:S(2)}) async-start(f32[4,1,32]{2,1,0:T(1,128)} %broadcast_in_dim.16), calls=%async_computation.2 | async-start | bytes 4096 | tf_op jit(solution)/shard_map/all_to_all | solution.py:19
  198.4 8.7 %all-to-all-start.3 = ((bf16[4,32,256]{2,1,0:T(8,128)(2,1)}), bf16[4,32,256]{2,1,0:T(8,128)(2,1)S(1)}, u32[]{:S(2)}, u32[]{:S(2)}) async-start(bf16[4,32,256]{2,1,0:T(8,128)(2,1)} %broadcast_in_dim.17), calls=%async_computation.3 | async-start | bytes 131072 | tf_op jit(solution)/shard_map/all_to_all | solution.py:19
  202.4 166.1 %all-reduce.4.cloned.1.call-start = ((), (), s32[]{:S(2)}) async-start(), calls=%async_computation.10 | async-start | bytes 524288 | tf_op jit(solution)/shard_map/psum | solution.py:100
  227.7 416.9 %all-reduce.6.cloned.1.call-start = ((), (), s32[]{:S(2)}) async-start(), calls=%async_computation.11 | async-start | bytes 524288 | tf_op jit(solution)/shard_map/psum | solution.py:100
  460.9 255.6 %all-gather.5.cloned.1.call-start = ((), (), s32[]{:S(2)}) async-start(), calls=%async_computation.12 | async-start | bytes 10485760 | tf_op jit(solution)/shard_map/all_gather | solution.py:108
  461.5 260.3 %copy-start.1 = (bf16[1024,1024]{1,0:T(8,128)(2,1)S(1)}, bf16[1024,1024]{1,0:T(8,128)(2,1)}, u32[]{:S(2)}) copy-start(bf16[1024,1024]{1,0:T(8,128)(2,1)} %all-gather.3.cloned.1.call-done) | copy-start | bytes 6291460
  711.4 24.7 %all-to-all-start.7 = ((bf16[32,32,256]{2,1,0:T(8,128)(2,1)}), bf16[32,32,256]{2,1,0:T(8,128)(2,1)S(1)}, u32[]{:S(2)}, u32[]{:S(2)}) async-start(bf16[32,32,256]{2,1,0:T(8,128)(2,1)} %broadcast_in_dim.19), calls=%async_computation.7 | async-start | bytes 1048576 | tf_op jit(solution)/shard_map/all_to_all | solution.py:19
  716.4 83.0 %reduce-scatter.2.cloned.1.call-start = ((), (), s32[]{:S(2)}) async-start(), calls=%async_computation.13 | async-start | bytes 5406720 | tf_op jit(solution)/shard_map/reduce_scatter | solution.py:45
  716.5 5.8 copy-start
Sparse Core Ops, SparseCore 0:
  10.4 134.4 all-gather.2
  227.8 140.6 all-reduce.3
  461.0 183.4 all-reduce.5
Sparse Core Ops, SparseCore 1:
  463.0 60.4 all-gather.4
  746.7 52.6 reduce-scatter.1
where the time goes:
time: 814 us; the launch traced here: 810 us
  waiting for transfers between devices  517 us (64%)
  other arithmetic  122 us (15%)
  blocking collectives  59.6 us (7%)
  starting transfers between devices  43.9 us (5%)
  matrix products  29.3 us (4%)
  local copies, waits for them, and re-layouts  19.8 us (2%)
  between operations  18.4 us (2%)
    psum x2, waiting for transfers between devices, body(): lax.psum(jnp.dot(image.T, image, precision=lax.Precision.HIGHEST), ('grp'...  323 us
    all_gather x1, waiting for transfers between devices, body(): group_rows = lax.all_gather(landmarks, 'row', axis=0, tiled=True)  123 us
    another operation x13, other arithmetic, body(): lower = jnp.linalg.cholesky(gram)  68.6 us
    reduce_scatter x1, waiting for transfers between devices, side_by_side(): lax.psum_scatter(both, axis, scatter_dimension=dim, tiled=True)  52.7 us
    all_to_all x4, starting transfers between devices, copy_for_each(): lax.all_to_all(jnp.broadcast_to(x[None], (devices, *x.shape)), axis, 0, 0...  43.2 us
    another operation x5, other arithmetic, body(): ortho = jax.scipy.linalg.solve_triangular(lower, image.T, lower=True).T  39.4 us
    all_to_all x2, blocking collectives, sum_at_owner(): blocks = lax.all_to_all(in_blocks(x, dim, devices), axis, 0, 0, tiled=True)  38.6 us
    all_to_all x2, blocking collectives, copy_for_each(): lax.all_to_all(jnp.broadcast_to(x[None], (devices, *x.shape)), axis, 0, 0...  20.9 us
  transfers between devices with their start and end apart: 9, of which 7 were waited for; matrix products, arithmetic and copies ran while one was open for 11% of the time, Pallas kernels for 0%

commit v1 on v0

--- a/solution.py
+++ b/solution.py
@@ -97,7 +97,12 @@
         image = sum_at_owner(
             jnp.dot(affinity, cross_basis, preferred_element_type=jnp.float32), "row", 0
         )
-        gram = lax.psum(jnp.dot(image.T, image, precision=lax.Precision.HIGHEST), ("grp", "row"))
+        gram = jnp.sum(
+            lax.all_gather(
+                jnp.dot(image.T, image, precision=lax.Precision.HIGHEST), ("grp", "row")
+            ),
+            axis=0,
+        )
         lower = jnp.linalg.cholesky(gram)
         ortho = jax.scipy.linalg.solve_triangular(lower, image.T, lower=True).T
         current = ortho.astype(jnp.bfloat16)

time: 814 us -> 1200 us (1.47)
  waiting for transfers between devices: 517 us -> 869 us
  other arithmetic: 122 us -> 156 us
    all_gather x0 -> x2, waiting for transfers between devices: none -> 675 us  [body(): lax.all_gather(jnp.dot(image.T, image, precision=lax.Precision.HIGHEST),...]
    psum x2 -> x0, waiting for transfers between devices: 323 us -> none  [body(): lax.psum(jnp.dot(image.T, image, precision=lax.Precision.HIGHEST), ('grp'...]
    reduce_sum x0 -> x2, other arithmetic: none -> 24.3 us  [body(): jnp.sum(lax.all_gather(jnp.dot(image.T, image, precision=lax.Precision.HI...]
  transfers between devices with their start and end apart: 9 -> 9, of which waited for: 7 -> 7; matrix products, arithmetic and copies ran while one was open for 11% -> 9% of each run, Pallas kernels for 0% -> 0%
where the time goes in v1:
time: 1200 us
  waiting for transfers between devices  869 us (72%)
  other arithmetic  156 us (13%)
  blocking collectives  62.1 us (5%)
  starting transfers between devices  46.2 us (4%)
  matrix products  31 us (3%)
  local copies, waits for them, and re-layouts  17.5 us (1%)
  between operations  17 us (1%)
    all_gather x2, waiting for transfers between devices, body(): lax.all_gather(jnp.dot(image.T, image, precision=lax.Precision.HIGHEST),...  675 us
    all_gather x1, waiting for transfers between devices, body(): group_rows = lax.all_gather(landmarks, 'row', axis=0, tiled=True)  123 us
    another operation x13, other arithmetic, body(): lower = jnp.linalg.cholesky(gram)  68.6 us
    reduce_scatter x1, waiting for transfers between devices, side_by_side(): lax.psum_scatter(both, axis, scatter_dimension=dim, tiled=True)  53.3 us
    another operation x5, other arithmetic, body(): ortho = jax.scipy.linalg.solve_triangular(lower, image.T, lower=True).T  50.8 us
    all_to_all x4, starting transfers between devices, copy_for_each(): lax.all_to_all(jnp.broadcast_to(x[None], (devices, *x.shape)), axis, 0, 0...  45.7 us
    all_to_all x2, blocking collectives, sum_at_owner(): blocks = lax.all_to_all(in_blocks(x, dim, devices), axis, 0, 0, tiled=True)  41.4 us
    reduce_sum x2, other arithmetic, body(): jnp.sum(lax.all_gather(jnp.dot(image.T, image, precision=lax.Precision.HI...  24.3 us
  transfers between devices with their start and end apart: 9, of which 7 were waited for; matrix products, arithmetic and copies ran while one was open for 9% of the time, Pallas kernels for 0%

profile of v1, /device:TPU:1, one launch (start us, length us, event | category | flops | bytes accessed | tf_op | source)
XLA Modules:
  0.0 1198.7 jit_solution(1376467979749651863)
XLA Ops:
  7.2 0.7 all-gather.7.cloned.1.call-update
  7.9 0.9 broadcast_in_dim.14
  8.8 12.2 %all_to_all.42 = bf16[4,32,1024]{2,1,0:T(8,128)(2,1)S(1)} all-to-all(bf16[4,32,1024]{2,1,0:T(8,128)(2,1)S(1)} %broadcast_in_dim.14), channel_id=1, replica_groups=mesh['grp'=4,'row'=32] {'grp'}, dimensions={0} | all-to-all | bytes 524288 | tf_op jit(solution)/shard_map/all_to_all | solution.py:19
  21.2 122.9 %all-gather.7.cloned.1.call-done = bf16[1024,1024]{1,0:T(8,128)(2,1)} async-done(((bf16[32,1024]{1,0:T(8,128)(2,1)}), bf16[1024,1024]{1,0:T(8,128)(2,1)}) %all-gather.7.cloned.1.call-update) | async-done | bytes 2097168 | tf_op jit(solution)/shard_map/all_gather | solution.py:85
  144.1 2.1 multiply_reduce_fusion.1
  146.2 2.4 fusion.38
  148.6 0.7 broadcast_in_dim.15
  149.3 6.2 all-to-all-start.1
  155.6 7.3 all-to-all-done.1
  163.0 0.6 broadcast_in_dim.16
  163.6 28.1 %all-to-all-start.2 = ((f32[4,1,32]{2,1,0:T(1,128)}), f32[4,1,32]{2,1,0:T(1,128)S(1)}, u32[]{:S(2)}, u32[]{:S(2)}) async-start(f32[4,1,32]{2,1,0:T(1,128)} %broadcast_in_dim.16), calls=%async_computation.2 | async-start | bytes 4096 | tf_op jit(solution)/shard_map/all_to_all | solution.py:19
  191.7 4.5 all-to-all-done.2
  196.2 1.4 broadcast_in_dim.17
  197.6 3.9 all-to-all-start.3
  201.9 4.4 all-to-all-done.3
  206.3 0.3 fusion.39
  206.6 19.0 %all_to_all.44 = f32[32,32,256]{2,1,0:T(8,128)S(1)} all-to-all(f32[32,32,256]{2,1,0:T(8,128)S(1)} %fusion.39), channel_id=1, replica_groups=mesh['grp'=4,'row'=32] {'row'}, dimensions={0} | all-to-all | bytes 2097152 | tf_op jit(solution)/shard_map/all_to_all | solution.py:38
  225.7 1.1 fusion.40
  226.9 0.7 all-gather.9.cloned.1.call-update
  227.6 0.4 all-gather.13.cloned.1.call-start
  228.0 339.4 %all-gather.11.cloned.1.call-done = f32[32768,256]{1,0:T(8,128)} async-done(((f32[256,256]{1,0:T(8,128)}), f32[32768,256]{1,0:T(8,128)}) %all-gather.11.cloned.1.call-update) | async-done | bytes 33554448 | tf_op jit(solution)/shard_map/all_gather | solution.py:101
  567.4 12.2 %reduce_sum.99 = f32[256,256]{1,0:T(8,128)S(1)} reduce(f32[128,256,256]{2,1,0:T(8,128)} %bitcast.96, f32[]{:T(128)} %constant.80.clone.1), dimensions={0}, to_apply=%region_5.0 | reduce | flops 8323072 | bytes 33816580 | tf_op jit(solution)/shard_map/reduce_sum | solution.py:100
  579.8 11.7 cholesky.130
  591.6 9.8 custom-call.15
  601.6 0.3 convolution_subtract_fusion.1
  601.9 11.7 cholesky.147
  613.6 0.7 compare_reduce_fusion.2
  615.8 4.1 while.4
  615.8 0.6 fusion.66
  616.4 1.4 bitcast_dynamic-update-slice_fusion.4
  617.9 0.6 fusion.66
  618.5 1.4 bitcast_dynamic-update-slice_fusion.4
  619.9 30.9 %custom-call.16 = f32[2,128,128]{1,2,0:T(8,128)S(1)} custom-call(f32[2,128,128]{2,1,0:T(8,128)S(1)} %get-tuple-element.18), custom_call_target="InvertDiagBlocksLowerTriangular" | custom-call | tf_op jit(solution)/shard_map/jit(_solve_triangular)/triangular_solve | solution.py:107
  651.5 8.5 all_to_all.43
  659.9 0.3 fusion.41
  660.2 22.4 %all_to_all.45 = f32[32,32,256]{2,1,0:T(8,128)S(1)} all-to-all(f32[32,32,256]{2,1,0:T(8,128)S(1)} %fusion.41), channel_id=1, replica_groups=mesh['grp'=4,'row'=32] {'row'}, dimensions={0} | all-to-all | bytes 2097152 | tf_op jit(solution)/shard_map/all_to_all | solution.py:38
  682.7 1.1 fusion.42
  683.9 5.1 multiply_reduce_fusion
  688.9 335.7 %all-gather.13.cloned.1.call-done = f32[32768,256]{1,0:T(8,128)} async-done(((f32[256,256]{1,0:T(8,128)}), f32[32768,256]{1,0:T(8,128)}) %all-gather.13.cloned.1.call-update) | async-done | bytes 33554448 | tf_op jit(solution)/shard_map/all_gather | solution.py:101
  1024.6 12.1 %reduce_sum.101 = f32[256,256]{1,0:T(8,128)S(1)} reduce(f32[128,256,256]{2,1,0:T(8,128)} %bitcast.97, f32[]{:T(128)} %constant.80.clone.1), dimensions={0}, to_apply=%region_11.14 | reduce | flops 8323072 | bytes 33816580 | tf_op jit(solution)/shard_map/reduce_sum | solution.py:100
  1036.9 11.7 cholesky.164
  1048.7 9.8 custom-call.17
  1058.5 0.2 constant_dynamic-update-slice_fusion.1
  1058.7 0.3 convolution_subtract_fusion
  1059.0 11.7 cholesky.181
  1070.8 0.6 compare_reduce_fusion
  1071.4 0.6 compare_reduce_fusion.1
  1073.4 4.0 while.5
  1073.4 0.6 fusion.67
  1074.0 1.4 bitcast_dynamic-update-slice_fusion.5
  1075.4 0.6 fusion.67
  1076.0 1.4 bitcast_dynamic-update-slice_fusion.5
  1077.4 19.9 %custom-call.18 = f32[2,128,128]{1,2,0:T(8,128)S(1)} custom-call(f32[2,128,128]{2,1,0:T(8,128)S(1)} %get-tuple-element.19), custom_call_target="InvertDiagBlocksLowerTriangular" | custom-call | tf_op jit(solution)/shard_map/jit(_solve_triangular)/triangular_solve | solution.py:107
  1097.8 2.4 gather_fusion
  1100.2 0.6 divide_convert_fusion
  1100.8 0.9 broadcast_in_dim.19
  1101.7 7.4 all-to-all-start.7
  1109.1 15.7 %fusion = (f32[4096]{0:T(1024)S(1)}, f32[1024,4096]{1,0:T(8,128)}) fusion(f32[4096]{0:T(1024)S(1)} %multiply_reduce_fusion, f32[1024]{0:T(1024)S(1)} %multiply_reduce_fusion.1, bf16[1024,1024]{1,0:T(8,128)(2,1)S(1)} %copy-done, bf16[4096,1024]{1,0:T(8,128)(2,1)} %all-gather.9.cloned.1.call-done), kind=kOutput, calls=%fused_computation.7 | convolution fusion | flops 8615096320 | bytes 27299840 | tf_op jit(solution)/shard_map/dot_general | solution.py:66
  1124.8 8.2 fusion.2
  1133.0 2.3 pad_maximum_fusion
  1135.3 53.3 %reduce-scatter.2.cloned.1.call-done = f32[1024,257]{0,1:T(8,128)} async-done(((f32[4096,257]{0,1:T(8,128)}), f32[1024,257]{0,1:T(8,128)}) %reduce-scatter.2.cloned.1.call-update) | async-done | bytes 1052688 | tf_op jit(solution)/shard_map/reduce_scatter | solution.py:45
  1188.6 0.8 slice_sqrt_fusion
  1189.3 1.3 fusion.8
  1190.7 1.3 copy.20
  (53 shorter events, 3.0 us)
Async XLA Ops:
  7.2 137.0 %all-gather.7.cloned.1.call-start = ((), (), s32[]{:S(2)}) async-start(), calls=%async_computation.9 | async-start | bytes 2162688 | tf_op jit(solution)/shard_map/all_gather | solution.py:85
  149.3 13.5 %all-to-all-start.1 = ((f32[32,1,1024]{2,1,0:T(1,128)}), f32[32,1,1024]{2,1,0:T(1,128)S(1)}, u32[]{:S(2)}, u32[]{:S(2)}) async-start(f32[32,1,1024]{2,1,0:T(1,128)} %broadcast_in_dim.15), calls=%async_computation.1 | async-start | bytes 262144 | tf_op jit(solution)/shard_map/all_to_all | solution.py:19
  163.6 32.6 %all-to-all-start.2 = ((f32[4,1,32]{2,1,0:T(1,128)}), f32[4,1,32]{2,1,0:T(1,128)S(1)}, u32[]{:S(2)}, u32[]{:S(2)}) async-start(f32[4,1,32]{2,1,0:T(1,128)} %broadcast_in_dim.16), calls=%async_computation.2 | async-start | bytes 4096 | tf_op jit(solution)/shard_map/all_to_all | solution.py:19
  197.6 8.7 all-to-all-start.3
  201.5 365.9 %all-gather.11.cloned.1.call-start = ((), (), s32[]{:S(2)}) async-start(), calls=%async_computation.12 | async-start | bytes 33816576 | tf_op jit(solution)/shard_map/all_gather | solution.py:101
  226.8 457.0 %all-gather.9.cloned.1.call-start = ((), (), s32[]{:S(2)}) async-start(), calls=%async_computation.10 | async-start | bytes 10485760 | tf_op jit(solution)/shard_map/all_gather | solution.py:113
  227.6 797.0 %all-gather.13.cloned.1.call-start = ((), (), s32[]{:S(2)}) async-start(), calls=%async_computation.13 | async-start | bytes 33816576 | tf_op jit(solution)/shard_map/all_gather | solution.py:101
  1024.6 84.5 %copy-start = (bf16[1024,1024]{1,0:T(8,128)(2,1)S(1)}, bf16[1024,1024]{1,0:T(8,128)(2,1)}, u32[]{:S(2)}) copy-start(bf16[1024,1024]{1,0:T(8,128)(2,1)} %all-gather.7.cloned.1.call-done) | copy-start | bytes 6291460
  1101.7 23.1 %all-to-all-start.7 = ((bf16[32,32,256]{2,1,0:T(8,128)(2,1)}), bf16[32,32,256]{2,1,0:T(8,128)(2,1)S(1)}, u32[]{:S(2)}, u32[]{:S(2)}) async-start(bf16[32,32,256]{2,1,0:T(8,128)(2,1)} %broadcast_in_dim.19), calls=%async_computation.7 | async-start | bytes 1048576 | tf_op jit(solution)/shard_map/all_to_all | solution.py:19
  1109.1 79.5 %reduce-scatter.2.cloned.1.call-start = ((), (), s32[]{:S(2)}) async-start(), calls=%async_computation.11 | async-start | bytes 5406720 | tf_op jit(solution)/shard_map/reduce_scatter | solution.py:45
Sparse Core Ops, SparseCore 0:
  9.6 134.4 all-gather.6
  227.0 340.4 all-gather.10
  569.1 63.3 all-gather.8
  683.9 340.6 all-gather.12
  1135.4 53.0 reduce-scatter.1
